TPU v7x, 32 devices: a whole 2x2x4 slice. The times are simulated.
32 devices in a mesh: groups: 2 (over y), seq: 4 (over z), slide: 2 (over x), head: 2 (over core).
Axes of the slice: x: 2, y: 2, z: 4, core: 2. Of those that a mesh axis runs over, the one named last changes fastest.
Arguments:
- latents: bfloat16 [1024, 1024], P(('groups', 'seq'), 'head'), parts along dimension 0, may hold values from -153 to 153
- tile_keys: bfloat16 [4, 1024, 1024], P(('groups', 'slide'), 'seq', 'head'), parts along dimension 0, may hold values from -6 to 6
- tile_values: bfloat16 [4, 1024, 1024], P(('groups', 'slide'), 'seq', 'head'), parts along dimension 0, may hold values from -24 to 24
- tile_mask: int32 [4, 8], P(('groups', 'slide'), 'seq'), parts along dimension 0, may hold values from 0 to 1, as said below
- latent_counts: int32 [4], P(('groups', 'slide')), parts along dimension 0, may hold values from 128 to 512
- out_weight: bfloat16 [1024, 1024], P('head'), may hold values from -0.1875 to 0.1875
- cotangent: bfloat16 [4, 512, 1024], P(('groups', 'slide'), 'seq'), parts along dimension 0, may hold values from -6 to 6
Outputs:
- pooled: bfloat16 [4, 512, 1024], P(('groups', 'slide'), 'seq', 'head'), parts along dimension 0
- grad_latents: float32 [1024, 1024], P(('groups', 'seq'), 'head'), parts along dimension 0
- grad_keys: bfloat16 [4, 1024, 1024], P(('groups', 'slide'), 'seq', 'head'), parts along dimension 0
- grad_values: bfloat16 [4, 1024, 1024], P(('groups', 'slide'), 'seq', 'head'), parts along dimension 0
There are 2 independent parts, one for each index of `groups`. A program takes and returns all parts, laid end to end along the dimension named above; an argument that names none is the same for every part. Nothing has to cross between parts.
Inputs may be any that keep to these rules, and one draw needn't show every extreme that they name: `tile_mask`: every slide has at least one block of 128 tiles marked 1.
All inputs are finite; a program needn't handle non-finite values.
Results may differ from a plain program's by a relative error of at most 0.035.
Values may be sent and summed in bfloat16 or wider, within the bound.
No kernel may reach another device: no remote copies, remote signals or barrier semaphores. Data moves between devices by JAX's collectives and lax.ppermute only.
A program may use at most 64 MiB of HBM per device.

v0:
```python
import jax
import jax.numpy as jnp
from jax import lax
from jax.sharding import PartitionSpec as P

HD = 64
BLOCK = 128
masked_score = -1e30


def body(latents, tile_keys, tile_values, tile_mask, latent_counts, out_weight, cotangent):
    local_rows = latents.shape[0]
    local_width = latents.shape[1]
    head_count = local_width // HD
    factor = HD ** (-0.5)
    queries = lax.all_gather(latents, "seq", axis=0, tiled=True)
    total_rows = queries.shape[0]
    first_row = lax.axis_index("seq") * local_rows
    every_row = lax.broadcasted_iota(jnp.int32, (total_rows, 1), 0)
    own_row = lax.broadcasted_iota(jnp.int32, (local_rows, 1), 0) + first_row
    tile_count = tile_keys.shape[1]
    key_block = tile_keys[0]
    value_block = tile_values[0]
    valid_tiles = jnp.broadcast_to(tile_mask[0][:, None] > 0, (tile_count // BLOCK, BLOCK)).reshape(
        1, tile_count
    )
    live_count = latent_counts[0]
    score_list = []
    for which_head in range(head_count):
        columns = slice(which_head * HD, (which_head + 1) * HD)
        raw_scores = (
            jnp.einsum(
                "qc,tc->qt",
                queries[:, columns],
                key_block[:, columns],
                preferred_element_type=jnp.float32,
            )
            * factor
        )
        score_list.append(jnp.where(valid_tiles, raw_scores, masked_score))
    local_top = jnp.stack([jnp.max(scored, axis=1) for scored in score_list], axis=1)
    row_top = lax.pmax(local_top, "seq")
    expo_list = []
    weighted_list = []
    total_list = []
    for which_head in range(head_count):
        columns = slice(which_head * HD, (which_head + 1) * HD)
        expos = jnp.where(
            valid_tiles,
            jnp.exp(score_list[which_head] - row_top[:, which_head : which_head + 1]),
            0.0,
        )
        expo_list.append(expos)
        total_list.append(jnp.sum(expos, axis=1))
        weighted_list.append(
            jnp.dot(
                expos.astype(jnp.bfloat16),
                value_block[:, columns],
                preferred_element_type=jnp.float32,
            )
        )
    partial_sums = jnp.concatenate(weighted_list, axis=1)
    partial_totals = jnp.stack(total_list, axis=1)
    weighted, totals = lax.psum((partial_sums, partial_totals), "seq")
    span = weighted.shape[0]
    attended = jnp.where(
        every_row < live_count,
        (weighted.reshape(span, head_count, HD) / totals[:, :, None]).reshape(span, local_width),
        0.0,
    ).astype(jnp.bfloat16)
    own_attended = lax.dynamic_slice_in_dim(attended, first_row, local_rows, 0)
    pooled_part = jnp.dot(own_attended, out_weight, preferred_element_type=jnp.float32)
    pooled_parts = [
        lax.psum_scatter(pooled_part.astype(jnp.bfloat16), "head", scatter_dimension=1, tiled=True)
    ]
    projected = jnp.einsum(
        "rd,cd->rc", cotangent[0], out_weight, preferred_element_type=jnp.float32
    )
    upstream = jnp.where(own_row < live_count, projected, 0.0).astype(jnp.bfloat16)
    upstream_all = lax.all_gather(upstream, "seq", axis=0, tiled=True)
    row_delta = jnp.sum(
        (upstream_all.astype(jnp.float32) * attended.astype(jnp.float32)).reshape(
            total_rows, head_count, HD
        ),
        axis=2,
    )
    query_list = []
    key_list = []
    value_list = []
    for which_head in range(head_count):
        columns = slice(which_head * HD, (which_head + 1) * HD)
        up_head = upstream_all[:, columns]
        weights = expo_list[which_head] / totals[:, which_head : which_head + 1]
        value_list.append(
            jnp.einsum(
                "qt,qc->tc",
                weights.astype(jnp.bfloat16),
                up_head,
                preferred_element_type=jnp.float32,
            )
        )
        grad_prob = jnp.einsum(
            "qc,tc->qt", up_head, value_block[:, columns], preferred_element_type=jnp.float32
        )
        grad_score = (
            weights * (grad_prob - row_delta[:, which_head : which_head + 1]) * factor
        ).astype(jnp.bfloat16)
        query_list.append(
            jnp.dot(grad_score, key_block[:, columns], preferred_element_type=jnp.float32)
        )
        key_list.append(
            jnp.einsum(
                "qt,qc->tc", grad_score, queries[:, columns], preferred_element_type=jnp.float32
            )
        )
    grad_rows = jnp.concatenate(query_list, axis=1)
    key_grads = [jnp.concatenate(key_list, axis=1).astype(jnp.bfloat16)]
    value_grads = [jnp.concatenate(value_list, axis=1).astype(jnp.bfloat16)]
    own_grad = lax.psum_scatter(
        grad_rows.astype(jnp.bfloat16), "seq", scatter_dimension=0, tiled=True
    )
    grad_latents = lax.psum(own_grad, "slide").astype(jnp.float32)
    return (
        jnp.stack(pooled_parts, axis=0),
        grad_latents,
        jnp.stack(key_grads, axis=0),
        jnp.stack(value_grads, axis=0),
    )


def solution(mesh):
    placed = (
        P(("groups", "seq"), "head"),
        P(("groups", "slide"), "seq", "head"),
        P(("groups", "slide"), "seq", "head"),
        P(("groups", "slide"), "seq"),
        P(("groups", "slide")),
        P("head", None),
        P(("groups", "slide"), "seq", None),
    )
    return jax.shard_map(
        body,
        mesh=mesh,
        in_specs=placed,
        out_specs=(
            P(("groups", "slide"), "seq", "head"),
            P(("groups", "seq"), "head"),
            P(("groups", "slide"), "seq", "head"),
            P(("groups", "slide"), "seq", "head"),
        ),
        check_vma=False,
    )
```

profile of v0, /device:TPU:0, one launch (start us, length us, event | category | flops | bytes accessed | tf_op | source)
XLA Modules:
  0.0 189.9 jit_solution(3926986250691564147)
XLA Ops:
  7.2 0.7 compare_bitcast_fusion
  8.0 17.7 %all_gather.6 = bf16[512,512]{1,0:T(8,128)(2,1)S(1)} all-gather(bf16[128,512]{1,0:T(8,128)(2,1)} %param.7), channel_id=1, replica_groups=mesh['groups'=2,'seq'=4,'slide'=2,'head'=2] {'seq'}, dimensions={0}, use_global_device_ids=true | all-gather | bytes 655360 | tf_op jit(solution)/shard_map/all_gather | solution.py:16
  26.6 1.0 fusion.230
  27.7 1.1 fusion.229
  28.8 1.1 fusion.228
  29.8 1.1 fusion.227
  30.9 1.1 fusion.226
  32.0 19.5 %pmax.7 = f32[512,8]{0,1:T(8,128)S(1)} all-reduce(f32[512,8]{0,1:T(8,128)S(1)} %stack.67), channel_id=1, replica_groups=mesh['groups'=2,'seq'=4,'slide'=2,'head'=2] {'seq'}, use_global_device_ids=true, to_apply=%region_8.9 | all-reduce | flops 4096 | bytes 32768 | tf_op jit(solution)/shard_map/pmax | solution.py:42
  51.6 2.0 %convolution_dynamic-update-slice_fusion.7 = f32[512,512]{0,1:T(8,128)} fusion(f32[512,256]{0,1:T(8,128)} %get-tuple-element.51, f32[512]{0:T(512)S(1)} %bitcast.205, pred[256]{0:T(512)(128)(4,1)S(1)} %broadcast_bitcast_fusion, bf16[256,512]{1,0:T(8,128)(2,1)S(1)} %bitcast.161), kind=kOutput, calls=%fused_computation.57 | convolution fusion | flops 17170432 | bytes 723456 | tf_op jit(solution)/shard_map/dot_general | solution.py:56
  53.6 0.9 convolution_dynamic-update-slice_fusion.6
  54.6 0.9 convolution_dynamic-update-slice_fusion.5
  55.6 0.9 convolution_dynamic-update-slice_fusion.4
  56.6 0.9 convolution_dynamic-update-slice_fusion.3
  57.5 0.9 convolution_dynamic-update-slice_fusion.2
  58.5 0.9 convolution_dynamic-update-slice_fusion.1
  59.4 0.9 convolution_dynamic-update-slice_fusion
  60.4 2.5 %fusion.97 = (f32[512]{0:T(512)S(1)}, f32[512]{0:T(512)S(1)}, f32[512]{0:T(512)S(1)}, f32[512]{0:T(512)S(1)}, f32[512]{0:T(512)S(1)}, /*index=5*/f32[512]{0:T(512)S(1)}, f32[512]{0:T(512)S(1)}, f32[512]{0:T(512)S(1)}) fusion(f32[512,256]{0,1:T(8,128)S(1)} %get-tuple-element.65, f32[512]{0:T(512)S(1)} %bitcast.182, ...), kind=kLoop, calls=%fused_computation.158 | loop fusion | flops 3141632 | bytes 4227328 | tf_op jit(solution)/shard_map/reduce_sum | solution.py:54
  63.5 1.4 fusion.32
  64.9 21.1 %all_gather.7 = bf16[512,512]{0,1:T(8,128)(2,1)S(1)} all-gather(bf16[128,512]{0,1:T(8,128)(2,1)S(1)} %fusion.32), channel_id=1, replica_groups=mesh['groups'=2,'seq'=4,'slide'=2,'head'=2] {'seq'}, dimensions={0}, use_global_device_ids=true | all-gather | bytes 655360 | tf_op jit(solution)/shard_map/all_gather | solution.py:80
  86.0 19.5 %psum.22 = f32[512,8]{0,1:T(8,128)S(1)} all-reduce(f32[512,8]{0,1:T(8,128)S(1)} %stack.76), channel_id=1, replica_groups=mesh['groups'=2,'seq'=4,'slide'=2,'head'=2] {'seq'}, use_global_device_ids=true, to_apply=%region_18.19 | all-reduce | flops 4096 | bytes 32768 | tf_op jit(solution)/shard_map/psum | solution.py:64
  105.6 2.0 %fusion.42 = bf16[1,256,512]{1,2,0:T(8,128)(2,1)} fusion(bf16[512,512]{0,1:T(8,128)(2,1)S(1)} %all_gather.7, f32[512,256]{0,1:T(8,128)} %get-tuple-element.51, f32[512]{0:T(512)S(1)} %bitcast.231, f32[512]{0:T(512)S(1)} %bitcast.207, pred[256]{0:T(512)(128)(4,1)S(1)} %broadcast_bitcast_fusion), kind=kOutput, calls=%fused_computation.92 | convolution fusion | flops 17317888 | bytes 627200 | tf_op jit(solution)/shard_map/qt,qc->tc/dot_general | solution.py:95
  107.6 0.9 fusion.44
  108.7 0.9 fusion.46
  109.7 0.9 fusion.48
  110.7 0.9 fusion.50
  111.8 0.9 fusion.52
  112.7 0.9 fusion.54
  113.6 0.9 fusion.56
  114.5 1.8 copy.46
  116.3 2.3 %bitcast_reduce_fusion = (f32[512,8]{0,1:T(8,128)S(1)}, bf16[512,512]{0,1:T(8,128)(2,1)}) fusion(bf16[512,512]{0,1:T(8,128)(2,1)S(1)} %all_gather.7, f32[512,512]{0,1:T(8,128)} %all-reduce.3.cloned.1.call-done, f32[512,8]{0,1:T(8,128)S(1)} %psum.22, pred[512]{0:T(512)(128)(4,1)S(1)} %iota_compare_fusion), kind=kLoop, calls=%fused_computation.123 | loop fusion | flops 1830912 | bytes 2130432 | tf_op jit(solution)/shard_map/reduce_sum | solution.py:81
  118.9 0.8 copy-done.15
  120.0 0.7 copy-done.12
  121.0 0.8 copy-done.9
  122.1 0.7 copy-done.6
  123.1 0.8 copy-done.3
  125.4 0.7 copy-done.29
  128.0 1.0 copy.56
  129.1 0.9 copy-done.21
  130.5 0.7 copy-done.25
  131.4 0.7 copy-done.27
  132.4 0.7 copy-done.33
  133.1 2.0 %convolution_convert_fusion = bf16[128,1024]{1,0:T(8,128)(2,1)} fusion(bf16[512,1024]{1,0:T(8,128)(2,1)S(1)} %copy-done, bf16[512,512]{0,1:T(8,128)(2,1)} %get-tuple-element.25, s32[]{:T(128)S(6)} %select_n.77), kind=kOutput, calls=%fused_computation.48 | convolution fusion | flops 134348800 | bytes 1441796 | tf_op jit(solution)/shard_map/dot_general | solution.py:72
  135.1 15.1 %reduce-scatter.7.cloned.1.call-done = bf16[128,512]{1,0:T(8,128)(2,1)} async-done(((bf16[512,512]{1,0:T(8,128)(2,1)}), bf16[128,512]{1,0:T(8,128)(2,1)}) %reduce-scatter.7.cloned.1.call-update) | async-done | bytes 131088
  150.2 1.7 copy.57
  153.7 0.9 copy.45
  154.5 18.5 %all-reduce.5.cloned.1.call-done = bf16[128,512]{0,1:T(8,128)(2,1)} async-done(((bf16[128,512]{0,1:T(8,128)(2,1)}), bf16[128,512]{0,1:T(8,128)(2,1)}) %all-reduce.5.cloned.1.call-update) | async-done | bytes 131088 | tf_op jit(solution)/shard_map/psum | solution.py:122
  173.0 1.7 copy.44
  174.7 8.7 %reduce-scatter.5.cloned.1.call-done = bf16[128,512]{1,0:T(8,128)(2,1)} async-done(((bf16[128,1024]{1,0:T(8,128)(2,1)}), bf16[128,512]{1,0:T(8,128)(2,1)}) %reduce-scatter.5.cloned.1.call-update) | async-done | bytes 131088 | tf_op jit(solution)/shard_map/reduce_scatter | solution.py:74
  (104 shorter events, 9.5 us)
Async XLA Ops:
  7.2 56.3 %copy-start = (bf16[512,1024]{1,0:T(8,128)(2,1)S(1)}, bf16[512,1024]{1,0:T(8,128)(2,1)}, u32[]{:S(2)}) copy-start(bf16[512,1024]{1,0:T(8,128)(2,1)} %param.12) | copy-start | bytes 3145732
  7.2 109.1 %all-reduce.3.cloned.1.call-start = ((), (), s32[]{:S(2)}) async-start(), calls=%async_computation.2 | async-start | bytes 2097152 | tf_op jit(solution)/shard_map/psum | solution.py:64
  8.0 17.7 %copy-start.28 = (bf16[1,256,512]{2,1,0:T(8,128)(2,1)S(1)}, bf16[1,256,512]{2,1,0:T(8,128)(2,1)}, u32[]{:S(2)}) copy-start(bf16[1,256,512]{2,1,0:T(8,128)(2,1)} %param.8) | copy-start | bytes 786436
  26.6 33.7 %copy-start.1 = (f32[512,256]{0,1:T(8,128)}, f32[512,256]{0,1:T(8,128)S(1)}, u32[]{:S(2)}) copy-start(f32[512,256]{0,1:T(8,128)S(1)} %get-tuple-element.61) | copy-start | bytes 1572868
  30.9 20.6 %copy-start.30 = (bf16[1,256,512]{2,1,0:T(8,128)(2,1)S(1)}, bf16[1,256,512]{2,1,0:T(8,128)(2,1)}, u32[]{:S(2)}) copy-start(bf16[1,256,512]{2,1,0:T(8,128)(2,1)} %param.9) | copy-start | bytes 786436
  51.6 2.0 %copy-start.13 = (f32[512,256]{0,1:T(8,128)S(1)}, f32[512,256]{0,1:T(8,128)}, u32[]{:S(2)}) copy-start(f32[512,256]{0,1:T(8,128)} %get-tuple-element.53) | copy-start | bytes 1572868
  53.6 1.0 copy-start.10
  54.5 1.1 copy-start.7
  55.6 1.1 copy-start.4
  60.3 89.9 %reduce-scatter.7.cloned.1.call-start = ((), (), s32[]{:S(2)}) async-start(), calls=%async_computation.5 | async-start | bytes 655360
  105.6 2.0 %copy-start.14 = (f32[512,256]{0,1:T(8,128)S(1)}, f32[512,256]{0,1:T(8,128)}, u32[]{:S(2)}) copy-start(f32[512,256]{0,1:T(8,128)} %get-tuple-element.53) | copy-start | bytes 1572868
  107.6 1.0 copy-start.11
  108.7 1.0 copy-start.8
  109.7 1.0 copy-start.5
  110.7 1.0 copy-start.2
  116.3 2.3 %copy-start.32 = (f32[512,256]{0,1:T(8,128)S(1)}, f32[512,256]{0,1:T(8,128)}, u32[]{:S(2)}) copy-start(f32[512,256]{0,1:T(8,128)} %get-tuple-element.51) | copy-start | bytes 1572868
  118.6 1.0 copy-start.15
  118.9 6.5 %copy-start.20 = (bf16[512,256]{0,1:T(8,128)(2,1)}, bf16[512,256]{0,1:T(8,128)(2,1)S(1)}, u32[]{:S(2)}) copy-start(bf16[512,256]{0,1:T(8,128)(2,1)S(1)} %fusion.31) | copy-start | bytes 786436
  119.7 1.0 copy-start.12
  120.0 6.3 %copy-start.22 = (bf16[512,256]{0,1:T(8,128)(2,1)}, bf16[512,256]{0,1:T(8,128)(2,1)S(1)}, u32[]{:S(2)}) copy-start(bf16[512,256]{0,1:T(8,128)(2,1)S(1)} %fusion.30) | copy-start | bytes 786436
  120.7 1.0 copy-start.9
  121.0 5.6 %copy-start.24 = (bf16[512,256]{0,1:T(8,128)(2,1)}, bf16[512,256]{0,1:T(8,128)(2,1)S(1)}, u32[]{:S(2)}) copy-start(bf16[512,256]{0,1:T(8,128)(2,1)S(1)} %fusion.29) | copy-start | bytes 786436
  121.8 1.0 copy-start.6
  122.1 4.7 %copy-start.26 = (bf16[512,256]{0,1:T(8,128)(2,1)}, bf16[512,256]{0,1:T(8,128)(2,1)S(1)}, u32[]{:S(2)}) copy-start(bf16[512,256]{0,1:T(8,128)(2,1)S(1)} %fusion.28) | copy-start | bytes 786436
  122.8 1.0 copy-start.3
  123.0 4.0 %copy-start.18 = (bf16[512,256]{0,1:T(8,128)(2,1)}, bf16[512,256]{0,1:T(8,128)(2,1)S(1)}, u32[]{:S(2)}) copy-start(bf16[512,256]{0,1:T(8,128)(2,1)S(1)} %fusion.27) | copy-start | bytes 786436
  123.8 0.9 copy-start.31
  124.1 3.1 %copy-start.16 = (bf16[512,256]{0,1:T(8,128)(2,1)}, bf16[512,256]{0,1:T(8,128)(2,1)S(1)}, u32[]{:S(2)}) copy-start(bf16[512,256]{0,1:T(8,128)(2,1)S(1)} %fusion.26) | copy-start | bytes 786436
  125.1 1.0 copy-start.29
  129.1 0.9 copy-start.21
  129.1 1.1 copy-start.23
  129.1 43.9 %all-reduce.5.cloned.1.call-start = ((), (), s32[]{:S(2)}) async-start(), calls=%async_computation.4 | async-start | bytes 262144 | tf_op jit(solution)/shard_map/psum | solution.py:122
  130.2 1.0 copy-start.25
  131.2 0.9 copy-start.27
  132.4 0.7 copy-start.33
  133.1 18.9 %copy-start.34 = (bf16[1,256,512]{1,2,0:T(8,128)(2,1)S(1)}, bf16[1,256,512]{1,2,0:T(8,128)(2,1)}, u32[]{:S(2)}) copy-start(bf16[1,256,512]{1,2,0:T(8,128)(2,1)} %copy-done.33) | copy-start | bytes 786436
  135.1 16.9 %copy-start.19 = (bf16[512,256]{0,1:T(8,128)(2,1)S(1)}, bf16[512,256]{0,1:T(8,128)(2,1)}, u32[]{:S(2)}) copy-start(bf16[512,256]{0,1:T(8,128)(2,1)} %copy-done.18) | copy-start | bytes 786436
  151.9 1.0 copy-start.17
  151.9 31.4 %reduce-scatter.5.cloned.1.call-start = ((), (), s32[]{:S(2)}) async-start(), calls=%async_computation.3 | async-start | bytes 393216 | tf_op jit(solution)/shard_map/reduce_scatter | solution.py:74
Sparse Core Ops, SparseCore 0:
  60.4 55.6 all-reduce.2
  129.2 20.9 reduce-scatter.6
  153.1 19.8 all-reduce.4
  175.6 7.7 reduce-scatter.4
where the time goes:
time: 191 us; the launch traced here: 190 us
  blocking collectives  77.8 us (41%)
  waiting for transfers between devices  42.7 us (22%)
  matrix products  32.4 us (17%)
  local copies, waits for them, and re-layouts  16.6 us (9%)
  between operations  14.8 us (8%)
  other arithmetic  5.53 us (3%)
    all_gather x1, blocking collectives, body(): upstream_all = lax.all_gather(upstream, 'seq', axis=0, tiled=True)  21.1 us
    psum x1, blocking collectives, body(): weighted, totals = lax.psum((partial_sums, partial_totals), 'seq')  19.5 us
    pmax x1, blocking collectives, body(): row_top = lax.pmax(local_top, 'seq')  19.5 us
    psum x1, waiting for transfers between devices, body(): grad_latents = lax.psum(own_grad, 'slide').astype(jnp.float32)  18.5 us
    all_gather x1, blocking collectives, body(): queries = lax.all_gather(latents, 'seq', axis=0, tiled=True)  17.7 us
    unnamed x75, local copies, waits for them, and re-layouts  16.4 us
    unnamed x5, waiting for transfers between devices  15.5 us
    reduce_scatter x1, waiting for transfers between devices, body(): lax.psum_scatter(pooled_part.astype(jnp.bfloat16), 'head', scatter_dimens...  8.71 us
  transfers between devices with their start and end apart: 4, of which 3 were waited for; matrix products, arithmetic and copies ran while one was open for 11% of the time, Pallas kernels for 0%

commit v1 on v0

--- a/solution.py
+++ b/solution.py
@@ -119,7 +119,7 @@
     own_grad = lax.psum_scatter(
         grad_rows.astype(jnp.bfloat16), "seq", scatter_dimension=0, tiled=True
     )
-    grad_latents = lax.psum(own_grad, "slide").astype(jnp.float32)
+    grad_latents = jnp.sum(lax.all_gather(own_grad, "slide"), axis=0).astype(jnp.float32)
     return (
         jnp.stack(pooled_parts, axis=0),
         grad_latents,

time: 191 us -> 172 us (0.901)
  waiting for transfers between devices: 42.7 us -> 15.1 us
  matrix products: 32.4 us -> 38.6 us
  blocking collectives: 77.8 us -> 83.5 us
  local copies, waits for them, and re-layouts: 16.6 us -> 13.1 us
    psum x1 -> x0, waiting for transfers between devices: 18.5 us -> none  [body(): grad_latents = lax.psum(own_grad, 'slide').astype(jnp.float32)]
    reduce_scatter x1, waiting for transfers between devices: 8.71 us -> 0.58 us  [body(): lax.psum_scatter(pooled_part.astype(jnp.bfloat16), 'head', scatter_dimens...]
    all_gather x0 -> x1, blocking collectives: none -> 5.67 us  [body(): lax.all_gather(own_grad, 'slide')]
    dot_general x8, matrix products: 1.97 us -> 6.92 us  [body(): jnp.dot(grad_score, key_block[:, columns], preferred_element_type=jnp.flo...]
    unnamed x75 -> x65, local copies, waits for them, and re-layouts: 16.4 us -> 12.8 us
    unnamed x5 -> x4, waiting for transfers between devices: 15.5 us -> 14.5 us
  transfers between devices with their start and end apart: 4 -> 3, of which waited for: 3 -> 2; matrix products, arithmetic and copies ran while one was open for 11% -> 12% of each run, Pallas kernels for 0% -> 0%
where the time goes in v1:
time: 172 us; the launch traced here: 171 us
  blocking collectives  83.5 us (49%)
  matrix products  38.6 us (22%)
  waiting for transfers between devices  15.1 us (9%)
  between operations  14.7 us (9%)
  local copies, waits for them, and re-layouts  13.1 us (8%)
  other arithmetic  6.22 us (4%)
    all_gather x1, blocking collectives, body(): upstream_all = lax.all_gather(upstream, 'seq', axis=0, tiled=True)  21.1 us
    psum x1, blocking collectives, body(): weighted, totals = lax.psum((partial_sums, partial_totals), 'seq')  19.5 us
    pmax x1, blocking collectives, body(): row_top = lax.pmax(local_top, 'seq')  19.5 us
    all_gather x1, blocking collectives, body(): queries = lax.all_gather(latents, 'seq', axis=0, tiled=True)  17.7 us
    unnamed x4, waiting for transfers between devices  14.5 us
    unnamed x65, local copies, waits for them, and re-layouts  12.8 us
    dot_general x8, matrix products, body(): jnp.dot(expos.astype(jnp.bfloat16), value_block[:, columns], preferred_el...  8.48 us
    dot_general x8, matrix products, body(): jnp.einsum('qt,qc->tc', weights.astype(jnp.bfloat16), up_head, preferred_...  8.28 us
  transfers between devices with their start and end apart: 3, of which 2 were waited for; matrix products, arithmetic and copies ran while one was open for 12% of the time, Pallas kernels for 0%

profile of v1, /device:TPU:0, one launch (start us, length us, event | category | flops | bytes accessed | tf_op | source)
XLA Modules:
  0.0 171.3 jit_solution(5143626990957413334)
XLA Ops:
  8.0 17.7 %all_gather.12 = bf16[512,512]{1,0:T(8,128)(2,1)S(1)} all-gather(bf16[128,512]{1,0:T(8,128)(2,1)} %param.7), channel_id=1, replica_groups=mesh['groups'=2,'seq'=4,'slide'=2,'head'=2] {'seq'}, dimensions={0}, use_global_device_ids=true | all-gather | bytes 655360 | tf_op jit(solution)/shard_map/all_gather | solution.py:16
  26.6 1.0 fusion.230
  27.7 1.1 fusion.229
  28.8 1.1 fusion.228
  29.8 1.1 fusion.227
  30.9 1.1 fusion.226
  32.0 19.5 %pmax.7 = f32[512,8]{0,1:T(8,128)S(1)} all-reduce(f32[512,8]{0,1:T(8,128)S(1)} %stack.67), channel_id=1, replica_groups=mesh['groups'=2,'seq'=4,'slide'=2,'head'=2] {'seq'}, use_global_device_ids=true, to_apply=%region_8.9 | all-reduce | flops 4096 | bytes 32768 | tf_op jit(solution)/shard_map/pmax | solution.py:42
  51.6 2.0 %convolution_dynamic-update-slice_fusion.7 = f32[512,512]{0,1:T(8,128)} fusion(f32[512,256]{0,1:T(8,128)} %get-tuple-element.51, f32[512]{0:T(512)S(1)} %bitcast.207, pred[256]{0:T(512)(128)(4,1)S(1)} %broadcast_bitcast_fusion, bf16[256,512]{1,0:T(8,128)(2,1)} %bitcast.163), kind=kOutput, calls=%fused_computation.57 | convolution fusion | flops 17170432 | bytes 723200 | tf_op jit(solution)/shard_map/dot_general | solution.py:56
  53.6 0.9 convolution_dynamic-update-slice_fusion.6
  54.7 0.9 convolution_dynamic-update-slice_fusion.5
  55.6 0.9 convolution_dynamic-update-slice_fusion.4
  56.6 0.9 convolution_dynamic-update-slice_fusion.3
  57.5 0.9 convolution_dynamic-update-slice_fusion.2
  58.5 0.9 convolution_dynamic-update-slice_fusion.1
  59.4 0.9 convolution_dynamic-update-slice_fusion
  60.4 2.5 %fusion.97 = (f32[512]{0:T(512)S(1)}, f32[512]{0:T(512)S(1)}, f32[512]{0:T(512)S(1)}, f32[512]{0:T(512)S(1)}, f32[512]{0:T(512)S(1)}, /*index=5*/f32[512]{0:T(512)S(1)}, f32[512]{0:T(512)S(1)}, f32[512]{0:T(512)S(1)}) fusion(f32[512,256]{0,1:T(8,128)S(1)} %get-tuple-element.65, f32[512]{0:T(512)S(1)} %bitcast.184, ...), kind=kLoop, calls=%fused_computation.158 | loop fusion | flops 3141632 | bytes 4227328 | tf_op jit(solution)/shard_map/reduce_sum | solution.py:54
  63.5 1.4 fusion.32
  64.9 21.1 %all_gather.13 = bf16[512,512]{0,1:T(8,128)(2,1)S(1)} all-gather(bf16[128,512]{0,1:T(8,128)(2,1)S(1)} %fusion.32), channel_id=1, replica_groups=mesh['groups'=2,'seq'=4,'slide'=2,'head'=2] {'seq'}, dimensions={0}, use_global_device_ids=true | all-gather | bytes 655360 | tf_op jit(solution)/shard_map/all_gather | solution.py:80
  86.0 19.5 %psum.15 = f32[512,8]{0,1:T(8,128)S(1)} all-reduce(f32[512,8]{0,1:T(8,128)S(1)} %stack.76), channel_id=1, replica_groups=mesh['groups'=2,'seq'=4,'slide'=2,'head'=2] {'seq'}, use_global_device_ids=true, to_apply=%region_18.19 | all-reduce | flops 4096 | bytes 32768 | tf_op jit(solution)/shard_map/psum | solution.py:64
  105.6 2.0 %fusion.42 = bf16[1,256,512]{1,2,0:T(8,128)(2,1)} fusion(bf16[512,512]{0,1:T(8,128)(2,1)S(1)} %all_gather.13, f32[512,256]{0,1:T(8,128)} %get-tuple-element.51, f32[512]{0:T(512)S(1)} %bitcast.233, f32[512]{0:T(512)S(1)} %bitcast.209, pred[256]{0:T(512)(128)(4,1)S(1)} %broadcast_bitcast_fusion), kind=kOutput, calls=%fused_computation.92 | convolution fusion | flops 17317888 | bytes 627200 | tf_op jit(solution)/shard_map/qt,qc->tc/dot_general | solution.py:95
  107.6 0.9 fusion.44
  108.7 0.9 fusion.46
  109.7 0.9 fusion.48
  110.8 0.9 fusion.50
  111.8 0.9 fusion.52
  112.7 0.9 fusion.54
  113.6 0.9 fusion.56
  114.5 1.8 %copy.44 = bf16[1,256,512]{2,1,0:T(8,128)(2,1)} copy(bf16[1,256,512]{1,2,0:T(8,128)(2,1)} %fusion.56) | data formatting | bytes 524288
  116.3 2.3 %bitcast_reduce_fusion = (f32[512,8]{0,1:T(8,128)S(1)}, bf16[512,512]{0,1:T(8,128)(2,1)}) fusion(bf16[512,512]{0,1:T(8,128)(2,1)S(1)} %all_gather.13, f32[512,512]{0,1:T(8,128)} %all-reduce.2.cloned.1.call-done, f32[512,8]{0,1:T(8,128)S(1)} %psum.15, pred[512]{0:T(512)(128)(4,1)S(1)} %iota_compare_fusion), kind=kLoop, calls=%fused_computation.123 | loop fusion | flops 1830912 | bytes 2130432 | tf_op jit(solution)/shard_map/reduce_sum | solution.py:81
  118.9 0.8 fusion.58
  119.8 0.8 fusion.40
  124.0 0.8 copy-done.3
  125.6 0.9 fusion.60
  126.6 0.9 fusion.39
  127.5 0.8 fusion.38
  128.3 0.9 fusion.37
  129.2 0.8 fusion.36
  130.0 0.9 fusion.35
  130.9 0.8 fusion.34
  131.8 0.9 fusion.33
  132.7 2.0 %copy.54 = bf16[512,512]{1,0:T(8,128)(2,1)} copy(bf16[512,512]{0,1:T(8,128)(2,1)} %fusion.33) | data formatting | bytes 1048576
  134.8 0.9 copy-done.17
  138.1 1.9 %convolution_convert_fusion = bf16[128,1024]{1,0:T(8,128)(2,1)} fusion(bf16[512,1024]{1,0:T(8,128)(2,1)S(1)} %copy-done, bf16[512,512]{0,1:T(8,128)(2,1)} %get-tuple-element.25, s32[]{:T(128)S(6)} %select_n.77), kind=kOutput, calls=%fused_computation.48 | convolution fusion | flops 134348800 | bytes 1441796 | tf_op jit(solution)/shard_map/dot_general | solution.py:72
  140.6 0.9 copy.43
  141.4 14.4 %reduce-scatter.7.cloned.1.call-done = bf16[128,512]{1,0:T(8,128)(2,1)} async-done(((bf16[512,512]{1,0:T(8,128)(2,1)}), bf16[128,512]{1,0:T(8,128)(2,1)}) %reduce-scatter.7.cloned.1.call-update) | async-done | bytes 131088
  155.9 1.0 copy.55
  156.9 5.7 %all-gather = bf16[256,512]{0,1:T(8,128)(2,1)S(1)} all-gather(bf16[128,512]{0,1:T(8,128)(2,1)S(1)} %copy.55), channel_id=2, replica_groups=mesh['groups'=2,'seq'=4,'slide'=2,'head'=2] {'slide'}, dimensions={0}, use_global_device_ids=true | all-gather | bytes 393216 | tf_op jit(solution)/shard_map/all_gather | solution.py:122
  163.3 0.8 copy.42
  (94 shorter events, 11.5 us)
Async XLA Ops:
  7.2 56.4 %copy-start = (bf16[512,1024]{1,0:T(8,128)(2,1)S(1)}, bf16[512,1024]{1,0:T(8,128)(2,1)}, u32[]{:S(2)}) copy-start(bf16[512,1024]{1,0:T(8,128)(2,1)} %param.12) | copy-start | bytes 3145732
  7.2 109.1 %all-reduce.2.cloned.1.call-start = ((), (), s32[]{:S(2)}) async-start(), calls=%async_computation.2 | async-start | bytes 2097152 | tf_op jit(solution)/shard_map/psum | solution.py:64
  8.0 17.7 %copy-start.24 = (bf16[1,256,512]{2,1,0:T(8,128)(2,1)S(1)}, bf16[1,256,512]{2,1,0:T(8,128)(2,1)}, u32[]{:S(2)}) copy-start(bf16[1,256,512]{2,1,0:T(8,128)(2,1)} %param.8) | copy-start | bytes 786436
  26.6 33.7 %copy-start.1 = (f32[512,256]{0,1:T(8,128)}, f32[512,256]{0,1:T(8,128)S(1)}, u32[]{:S(2)}) copy-start(f32[512,256]{0,1:T(8,128)S(1)} %get-tuple-element.61) | copy-start | bytes 1572868
  51.6 2.1 %copy-start.13 = (f32[512,256]{0,1:T(8,128)S(1)}, f32[512,256]{0,1:T(8,128)}, u32[]{:S(2)}) copy-start(f32[512,256]{0,1:T(8,128)} %get-tuple-element.53) | copy-start | bytes 1572868
  51.6 2.0 %copy-start.26 = (bf16[1,256,512]{2,1,0:T(8,128)(2,1)S(1)}, bf16[1,256,512]{2,1,0:T(8,128)(2,1)}, u32[]{:S(2)}) copy-start(bf16[1,256,512]{2,1,0:T(8,128)(2,1)} %param.9) | copy-start | bytes 786436
  53.6 1.0 copy-start.10
  54.6 1.1 copy-start.7
  55.6 1.1 copy-start.4
  60.3 95.6 %reduce-scatter.7.cloned.1.call-start = ((), (), s32[]{:S(2)}) async-start(), calls=%async_computation.4 | async-start | bytes 655360
  105.6 2.0 %copy-start.14 = (f32[512,256]{0,1:T(8,128)S(1)}, f32[512,256]{0,1:T(8,128)}, u32[]{:S(2)}) copy-start(f32[512,256]{0,1:T(8,128)} %get-tuple-element.53) | copy-start | bytes 1572868
  107.6 1.0 copy-start.11
  108.7 1.0 copy-start.8
  109.7 1.0 copy-start.5
  110.8 1.0 copy-start.2
  116.3 2.4 %copy-start.27 = (bf16[1,256,512]{2,1,0:T(8,128)(2,1)S(1)}, bf16[1,256,512]{2,1,0:T(8,128)(2,1)}, u32[]{:S(2)}) copy-start(bf16[1,256,512]{2,1,0:T(8,128)(2,1)} %param.9) | copy-start | bytes 786436
  116.3 2.4 %copy-start.28 = (f32[512,256]{0,1:T(8,128)S(1)}, f32[512,256]{0,1:T(8,128)}, u32[]{:S(2)}) copy-start(f32[512,256]{0,1:T(8,128)} %get-tuple-element.51) | copy-start | bytes 1572868
  118.9 1.7 copy-start.15
  120.6 1.0 copy-start.12
  121.6 1.0 copy-start.9
  121.9 5.6 %copy-start.16 = (bf16[512,256]{0,1:T(8,128)(2,1)}, bf16[512,256]{0,1:T(8,128)(2,1)S(1)}, u32[]{:S(2)}) copy-start(bf16[512,256]{0,1:T(8,128)(2,1)S(1)} %fusion.29) | copy-start | bytes 786436
  122.7 1.0 copy-start.6
  123.0 5.3 %copy-start.18 = (bf16[512,256]{0,1:T(8,128)(2,1)}, bf16[512,256]{0,1:T(8,128)(2,1)S(1)}, u32[]{:S(2)}) copy-start(bf16[512,256]{0,1:T(8,128)(2,1)S(1)} %fusion.28) | copy-start | bytes 786436
  123.7 1.0 copy-start.3
  124.0 5.2 %copy-start.20 = (bf16[512,256]{0,1:T(8,128)(2,1)}, bf16[512,256]{0,1:T(8,128)(2,1)S(1)}, u32[]{:S(2)}) copy-start(bf16[512,256]{0,1:T(8,128)(2,1)S(1)} %fusion.27) | copy-start | bytes 786436
  125.1 5.0 %copy-start.22 = (bf16[512,256]{0,1:T(8,128)(2,1)}, bf16[512,256]{0,1:T(8,128)(2,1)S(1)}, u32[]{:S(2)}) copy-start(bf16[512,256]{0,1:T(8,128)(2,1)S(1)} %fusion.26) | copy-start | bytes 786436
  125.6 1.0 copy-start.25
  134.7 0.9 copy-start.17
  134.7 1.0 copy-start.29
  134.7 1.2 copy-start.19
  134.7 30.0 %reduce-scatter.5.cloned.1.call-start = ((), (), s32[]{:S(2)}) async-start(), calls=%async_computation.3 | async-start | bytes 393216 | tf_op jit(solution)/shard_map/reduce_scatter | solution.py:74
  135.9 1.0 copy-start.21
  136.9 0.9 copy-start.23
Sparse Core Ops, SparseCore 0:
  60.4 55.6 all-reduce.1
  134.9 20.9 reduce-scatter.6
  158.7 5.9 reduce-scatter.4
